TPU v7x, 256 devices: a 2x2x32 block of a 4x8x32 slice. The times are simulated.
256 devices in a mesh: groups: 4 (over x, y), seq: 32 (over z), pd: 2 (over core).
Axes of the slice: x: 2, y: 2, z: 32, core: 2. Of those that a mesh axis runs over, the one named last changes fastest.
The devices are a block of a 4x8x32 slice.
Arguments:
- streams: bfloat16 [32768, 4, 7168], P(('groups', 'seq'), None, 'pd'), parts along dimension 0, may hold values from -6 to 6
- mix_first: bfloat16 [4, 7168, 24], P(None, 'pd'), may hold values from -0.03125 to 0.03125
- first_layer_bias: float32 [24], replicated, may hold values from -3 to 3
- pre_second: bfloat16 [4, 7168, 4], P(None, 'pd'), may hold values from -0.03125 to 0.03125
- bias_second: float32 [4], replicated, may hold values from -3 to 3
- w_latent: bfloat16 [2, 7168, 576], P(None, ('pd', 'seq')), may hold values from -0.0625 to 0.0625
- latent_gain: float32 [2, 512], replicated, may hold values from 0.5 to 1.5
- out_weight: bfloat16 [512, 7168], P(None, 'pd'), may hold values from -0.25 to 0.25
- span_slot: int32 [256], P('groups'), parts along dimension 0, may hold values from 0 to 63, each once
- block_owner: int32 [128], P('groups'), parts along dimension 0, may hold values from 0 to 31, each once
- prompt_length: int32 [4], P('groups'), parts along dimension 0, may hold values from 4096 to 8192
Outputs:
- cache: bfloat16 [2, 32768, 576], P(None, ('groups', 'seq')), parts along dimension 1
There are 4 independent parts, one for each index of `groups`. A program takes and returns all parts, laid end to end along the dimension named above; an argument that names none is the same for every part. Nothing has to cross between parts.
Inputs may be any that keep to these rules, and one draw needn't show every extreme that they name: span_slot is a permutation; slot q lies in rows q * 128 to q * 128 + 127 of streams. block_owner is a permutation.
All inputs are finite; a program needn't handle non-finite values.
Results may differ from a plain program's by a relative error of at most 0.0058.
Values may be sent and summed in bfloat16 or wider, within the bound.
A program may use at most 128 MiB of HBM per device.

v0:
```python
import jax
import jax.numpy as jnp
from jax import lax
from jax.sharding import PartitionSpec as P

LAT = 512
ROPE = 64
RESIDUAL_WAYS = 4
SINK = 20
EPSILON = 1e-06
THETA = 10000.0


def sent_to_all(x, axis):
    copies = jnp.broadcast_to(x, (lax.axis_size(axis), *x.shape))
    return lax.all_to_all(copies, axis, split_axis=0, concat_axis=0, tiled=True)


def taken_together(x, axis):
    return sent_to_all(x, axis).sum(axis=0)


def packed_total(arrays, axis):
    ends = [0]
    for a in arrays:
        ends.append(ends[-1] + a.size)
    so_far = taken_together(jnp.concatenate([a.ravel() for a in arrays]), axis)
    return tuple((so_far[b:e].reshape(a.shape) for a, b, e in zip(arrays, ends, ends[1:])))


def doubly_stochastic_normalize(blend_scores_raw):

    def one_sweep(turn_index, matrix):
        matrix = matrix / jnp.sum(matrix, axis=2, keepdims=True)
        return matrix / jnp.sum(matrix, axis=1, keepdims=True)

    return lax.fori_loop(0, SINK, one_sweep, jnp.exp(blend_scores_raw))


def combine(weights, stream_block):
    weighted = weights[:, 0, None] * stream_block[:, 0, :].astype(jnp.float32)
    for stream_index in range(1, RESIDUAL_WAYS):
        weighted = weighted + weights[:, stream_index, None] * stream_block[
            :, stream_index, :
        ].astype(jnp.float32)
    return weighted


def coefficients(stream_block, weights, offsets):
    flattened = stream_block.reshape(stream_block.shape[0], -1)
    partial_value = jnp.dot(
        flattened, weights.reshape(flattened.shape[1], -1), preferred_element_type=jnp.float32
    )
    elementwise_power_two = jnp.sum(jnp.square(flattened.astype(jnp.float32)), axis=1)
    projected, square_sum = packed_total((partial_value, elementwise_power_two), "pd")
    entry_count = flattened.shape[1] * lax.axis_size("pd")
    rms_scale = jnp.sqrt(square_sum / entry_count + EPSILON)
    return projected / rms_scale[:, None] + offsets[None, :]


def cache_entry(summed, places, gain_row):
    latent = summed[:, :LAT]
    mean_square = jnp.mean(latent * latent, axis=1, keepdims=True)
    normed = latent * lax.rsqrt(mean_square + EPSILON) * gain_row[None, :]
    half_rope = ROPE // 2
    frequency = THETA ** (-jnp.arange(half_rope, dtype=jnp.float32) / half_rope)
    angles = places.astype(jnp.float32)[:, None] * frequency[None, :]
    first_half = summed[:, LAT : LAT + half_rope]
    second = summed[:, LAT + half_rope :]
    cosine_table = jnp.cos(angles)
    sine_values = jnp.sin(angles)
    rotated = jnp.concatenate(
        [
            first_half * cosine_table - second * sine_values,
            second * cosine_table + first_half * sine_values,
        ],
        axis=1,
    )
    return jnp.concatenate([normed, rotated], axis=1).astype(jnp.bfloat16)


def on_device(
    streams,
    mix_first,
    first_layer_bias,
    pre_second,
    bias_second,
    w_latent,
    latent_gain,
    out_weight,
    span_slot,
    block_owner,
    prompt_length,
):
    tokens_here = streams.shape[0]
    span_rows = tokens_here // 2
    seq_count = lax.axis_size("seq")
    my_index = lax.axis_index("seq")
    own_slots = 2 * my_index + jnp.arange(2, dtype=jnp.int32)
    span_ids = jnp.arange(2 * seq_count, dtype=jnp.int32)
    own_spans = jnp.sum(
        span_ids[None, :] * (span_slot[None, :] == own_slots[:, None]).astype(jnp.int32), axis=1
    )
    places = (
        own_spans[:, None] * span_rows + jnp.arange(span_rows, dtype=jnp.int32)[None, :]
    ).reshape(-1)
    in_prompt = places < prompt_length[0]
    my_block = jnp.sum(
        jnp.arange(seq_count, dtype=jnp.int32) * (block_owner == my_index).astype(jnp.int32)
    )
    wanted_slots = span_slot[2 * my_block + jnp.arange(2, dtype=jnp.int32)]

    def latent_of(hidden, layer_index):
        partial_value = jnp.dot(
            hidden,
            lax.all_gather(w_latent[layer_index], "seq", axis=0, tiled=True),
            preferred_element_type=jnp.float32,
        )
        summed = taken_together(partial_value, "pd")
        return cache_entry(summed, places, latent_gain[layer_index])

    def masked(entry_rows):
        return jnp.where(in_prompt[:, None], entry_rows, jnp.zeros((), jnp.bfloat16))

    blend_weight = coefficients(streams, mix_first, first_layer_bias)
    pre_gate = jax.nn.sigmoid(blend_weight[:, :RESIDUAL_WAYS])
    post_gate = 2.0 * jax.nn.sigmoid(blend_weight[:, RESIDUAL_WAYS : 2 * RESIDUAL_WAYS])
    residual_blend_matrix = doubly_stochastic_normalize(
        blend_weight[:, 2 * RESIDUAL_WAYS :].reshape(-1, RESIDUAL_WAYS, RESIDUAL_WAYS)
    )
    hidden = combine(pre_gate, streams).astype(jnp.bfloat16)
    entry_first = latent_of(hidden, 0)
    branch = jnp.dot(entry_first[:, :LAT], out_weight, preferred_element_type=jnp.float32)
    updated = jnp.stack(
        [
            combine(residual_blend_matrix[:, stream_index, :], streams)
            + post_gate[:, stream_index, None] * branch
            for stream_index in range(RESIDUAL_WAYS)
        ],
        axis=1,
    ).astype(jnp.bfloat16)
    second_coef = coefficients(updated, pre_second, bias_second)
    hidden_second = combine(jax.nn.sigmoid(second_coef), updated).astype(jnp.bfloat16)
    entry_second = latent_of(hidden_second, 1)
    stacked = jnp.stack([masked(entry_first), masked(entry_second)])
    collected = jnp.zeros_like(stacked)
    shard_piece = lax.all_gather(stacked, "seq", axis=1, tiled=True)
    piece_rows = shard_piece.shape[1]
    span_parts = []
    for lane in range(2):
        offset = wanted_slots[lane] * span_rows
        inside = jnp.logical_and(offset >= 0, offset + span_rows <= piece_rows)
        clipped = jnp.clip(offset, 0, piece_rows - span_rows)
        sliced = lax.dynamic_slice_in_dim(shard_piece, clipped, span_rows, 1)
        span_parts.append(
            jnp.where(inside, sliced, collected[:, lane * span_rows : (lane + 1) * span_rows])
        )
    return jnp.concatenate(span_parts, axis=1)


def solution(mesh):
    placed = (
        P(("groups", "seq"), None, "pd"),
        P(None, "pd", None),
        P(),
        P(None, "pd", None),
        P(),
        P(None, ("pd", "seq"), None),
        P(),
        P(None, "pd"),
        P("groups"),
        P("groups"),
        P("groups"),
    )
    return jax.shard_map(
        on_device,
        mesh=mesh,
        in_specs=placed,
        out_specs=P(None, ("groups", "seq"), None),
        check_vma=False,
    )
```

profile of v0, /device:TPU:38, one launch (start us, length us, event | category | flops | bytes accessed | tf_op | source)
XLA Modules:
  0.0 583.2 jit_solution(3354800891817134645)
XLA Ops:
  6.5 0.0 copy-start
  6.6 1.8 fusion.78
  8.3 0.1 all-gather.8.cloned.1.call-update
  8.4 0.0 copy-done
  8.4 5.2 convolution_bitcast_fusion
  13.6 0.1 reshape.292
  13.7 0.0 copy-start.7
  13.7 8.0 %multiply_reduce_fusion.1 = f32[256]{0:T(256)S(1)} fusion(bf16[256,4,3584]{2,1,0:T(4,128)(2,1)} %param.13), kind=kLoop, calls=%fused_computation.4 | loop fusion | flops 11009792 | bytes 7341056 | tf_op jit(solution)/shard_map/reduce_sum | solution.py:54
  21.7 0.6 broadcast_in_dim.23
  22.4 3.3 all-to-all-start
  25.7 0.1 all-gather.10.cloned.1.call-start
  25.8 0.7 all-gather.10.cloned.1.call-update
  26.5 0.1 all-gather.6.cloned.1.call-start
  26.6 0.5 all-to-all-done
  27.1 0.1 reduce_sum.111
  27.2 0.1 reshape.293
  27.3 0.1 copy.68
  27.4 0.1 divide_add_fusion
  27.5 1.7 while.10
  29.2 0.0 copy-start.2
  29.2 0.0 copy-start.6
  29.3 7.4 %copy.65 = bf16[256,4,3584]{2,0,1:T(8,128)(2,1)} copy(bf16[256,4,3584]{2,1,0:T(4,128)(2,1)} %param.13) | data formatting | bytes 14680064 | tf_op args[0]
  37.3 0.2 fusion.67
  37.5 0.1 compare_bitcast_fusion
  37.6 0.1 convert_bitcast_fusion
  37.7 121.9 %all-gather.8.cloned.1.call-done = bf16[1,3584,576]{2,1,0:T(8,128)(2,1)} async-done(((bf16[1,112,576]{2,1,0:T(8,128)(2,1)}), bf16[1,3584,576]{2,1,0:T(8,128)(2,1)}) %all-gather.8.cloned.1.call-update) | async-done | bytes 4128784 | tf_op jit(solution)/shard_map/all_gather | solution.py:116
  159.6 8.4 %fusion.2 = f32[256,576]{0,1:T(8,128)S(1)} fusion(bf16[1,3584,576]{2,1,0:T(8,128)(2,1)} %all-gather.8.cloned.1.call-done, f32[256]{0:T(256)S(1)} %bitcast.168, f32[256]{0:T(256)S(1)} %bitcast.167, f32[256]{0:T(256)S(1)} %bitcast.166, f32[256]{0:T(256)S(1)} %bitcast.169, bf16[256,4,3584]{2,0,1:T(8,128)(2,1)} %copy.65), kind=kOutput, calls=%fused_computation.28 | convolution fusion | flops 1067974656 | bytes 12062720 | tf_op jit(solution)/shard_map/dot_general | solution.py:114
  168.0 0.1 broadcast_in_dim.24
  168.1 4.7 all_to_all.22
  172.8 0.1 reduce_sum.112
  173.0 0.1 multiply_reduce_fusion.3
  173.1 0.0 slice-start.1
  173.1 7.9 %fusion.12 = (bf16[256,3584]{1,0:T(8,128)(2,1)S(1)}, bf16[256,3584]{1,0:T(8,128)(2,1)S(1)}, f32[256,3584]{1,0:T(8,128)S(1)}) fusion(f32[256]{0:T(256)S(1)} %bitcast.160, f32[256]{0:T(256)S(1)} %bitcast.163, f32[256]{0:T(256)S(1)} %bitcast.164, f32[256]{0:T(256)S(1)} %bitcast.165, f32[256]{0:T(256)S(1)} %bitcast.162, bf16[256,4,3584]{2,0,1:T(8,128)(2,1)} %copy.65, ...), kind=kOutput, calls=%fused_computation.38 | convolution fusion | flops 961937408 | bytes 18887680 | tf_op jit(solution)/shard_map/dot_general | solution.py:133
  181.0 0.0 copy-start.9
  181.0 4.1 fusion.17
  185.2 1.2 copy-done.3
  186.4 2.0 fusion.38
  188.5 0.1 reshape.294
  188.6 0.0 copy-start.8
  188.6 4.0 multiply_reduce_fusion
  192.7 3.7 all_to_all.23
  196.4 0.1 reshape.295
  196.6 0.1 copy.75
  196.6 0.0 copy-done.8
  196.7 0.1 add_divide_fusion
  196.8 0.1 fusion.76
  196.9 95.3 %all-gather.10.cloned.1.call-done = bf16[1,3584,576]{2,1,0:T(8,128)(2,1)} async-done(((bf16[1,112,576]{2,1,0:T(8,128)(2,1)}), bf16[1,3584,576]{2,1,0:T(8,128)(2,1)}) %all-gather.10.cloned.1.call-update) | async-done | bytes 4128784 | tf_op jit(solution)/shard_map/all_gather | solution.py:116
  292.2 6.6 %fusion = f32[256,576]{0,1:T(8,128)S(1)} fusion(bf16[1,3584,576]{2,1,0:T(8,128)(2,1)} %all-gather.10.cloned.1.call-done, bf16[256,3584]{1,0:T(8,128)(2,1)} %copy-done.5, bf16[256,3584]{1,0:T(8,128)(2,1)} %copy-done.3, bf16[256,3584]{1,0:T(8,128)(2,1)S(1)} %get-tuple-element.28, bf16[256,3584]{1,0:T(8,128)(2,1)} %copy-done.4, f32[256]{0:T(256)S(1)} %bitcast.175, ...), kind=kOutput, calls=%fused_computation.26 | convolution fusion | flops 1067974656 | bytes 12062720 | tf_op jit(solution)/shard_map/dot_general | solution.py:114
  298.8 0.1 broadcast_in_dim.27
  298.9 4.7 all_to_all.24
  303.6 0.1 reduce_sum.116
  303.7 0.1 multiply_reduce_fusion.2
  303.8 0.1 fusion.39
  304.0 0.2 fusion.59
  304.2 0.1 maximum_select_fusion
  304.3 0.9 pad_maximum_fusion.4
  305.2 0.1 all-gather.6.cloned.1.call-update
  305.2 0.7 fusion.72
  306.7 0.6 gather_fusion
  307.3 0.6 fusion.87
  309.2 265.1 %all-gather.6.cloned.1.call-done = bf16[2,8192,576]{1,2,0:T(8,128)(2,1)} async-done(((bf16[2,256,576]{1,2,0:T(8,128)(2,1)}), bf16[2,8192,576]{1,2,0:T(8,128)(2,1)}) %all-gather.6.cloned.1.call-update) | async-done | bytes 18874384 | tf_op jit(solution)/shard_map/all_gather | solution.py:147
  574.3 1.5 dynamic-slice_select_fusion.1
  575.8 0.9 pad_maximum_fusion.5
  576.7 0.0 copy-done.1
  (101 shorter events, 1.5 us)
Async XLA Ops:
  6.5 1.9 copy-start
  6.6 153.1 %all-gather.8.cloned.1.call-start = ((), (), s32[]{:S(2)}) async-start(), calls=%async_computation.5 | async-start | bytes 4730880 | tf_op jit(solution)/shard_map/all_gather | solution.py:116
  13.7 13.6 %copy-start.7 = (f32[24]{0:T(128)S(1)}, f32[24]{0:T(128)}, u32[]{:S(2)}) copy-start(f32[24]{0:T(128)} %param.15) | copy-start | bytes 292
  22.4 4.7 all-to-all-start
  25.7 266.6 %all-gather.10.cloned.1.call-start = ((), (), s32[]{:S(2)}) async-start(), calls=%async_computation.6 | async-start | bytes 4730880 | tf_op jit(solution)/shard_map/all_gather | solution.py:116
  26.5 547.8 %all-gather.6.cloned.1.call-start = ((), (), s32[]{:S(2)}) async-start(), calls=%async_computation.4 | async-start | bytes 19464192 | tf_op jit(solution)/shard_map/all_gather | solution.py:147
  29.2 8.0 %copy-start.2 = (s32[64]{0:T(128)S(1)}, s32[64]{0:T(128)}, u32[]{:S(2)}) copy-start(s32[64]{0:T(128)} %param.21) | copy-start | bytes 772
  29.2 8.4 %copy-start.6 = (f32[2,512]{1,0:T(2,128)S(1)}, f32[2,512]{1,0:T(2,128)}, u32[]{:S(2)}) copy-start(f32[2,512]{1,0:T(2,128)} %param.19) | copy-start | bytes 12292
  173.1 7.9 %slice-start = ((s8[7340032]{0:T(1024)(128)(4,1)}), s8[4194304]{0:T(1024)(128)(4,1)S(1)}, s32[]{:S(2)}) async-start(s8[7340032]{0:T(1024)(128)(4,1)} %bitcast.137), calls=%async_computation.7 | async-start | bytes 8388608
  173.1 7.9 %slice-start.1 = ((s8[7340032]{0:T(1024)(128)(4,1)}), s8[3145728]{0:T(1024)(128)(4,1)S(1)}, s32[]{:S(2)}) async-start(s8[7340032]{0:T(1024)(128)(4,1)} %bitcast.137), calls=%async_computation.8 | async-start | bytes 6291456
  181.0 4.2 copy-start.4
  181.0 4.2 copy-start.5
  181.0 5.4 copy-start.9
  185.2 1.2 copy-start.3
  188.6 8.1 %copy-start.8 = (f32[4]{0:T(128)S(1)}, f32[4]{0:T(128)}, u32[]{:S(2)}) copy-start(f32[4]{0:T(128)} %param.17) | copy-start | bytes 52
  303.6 1.6 copy-start.10
  303.6 273.1 %copy-start.1 = (bf16[4,3584,24]{1,2,0:T(8,128)(2,1)S(1)}, bf16[4,3584,24]{1,2,0:T(8,128)(2,1)}, u32[]{:S(2)}) copy-start(bf16[4,3584,24]{1,2,0:T(8,128)(2,1)} %param.14) | copy-start | bytes 2064388
Sparse Core Ops, SparseCore 0:
  9.1 150.4 all-gather.7
  161.4 130.7 all-gather.9
  305.4 268.8 all-gather.5
where the time goes:
time: 584 us; the launch traced here: 583 us
  waiting for transfers between devices  484 us (83%)
  matrix products  30.1 us (5%)
  other arithmetic  23.1 us (4%)
  between operations  16.2 us (3%)
  local copies, waits for them, and re-layouts  13.2 us (2%)
  blocking collectives  13.1 us (2%)
    all_gather x1, waiting for transfers between devices, on_device(): shard_piece = lax.all_gather(stacked, 'seq', axis=1, tiled=True)  265 us
    all_gather x2, waiting for transfers between devices, latent_of(): lax.all_gather(w_latent[layer_index], 'seq', axis=0, tiled=True)  217 us
    dot_general x2, matrix products, latent_of(): jnp.dot(hidden, lax.all_gather(w_latent[layer_index], 'seq', axis=0, tile...  15 us
    all_to_all x3, blocking collectives, sent_to_all(): return lax.all_to_all(copies, axis, split_axis=0, concat_axis=0, tiled=True)  13.1 us
    reduce_sum x2, other arithmetic, coefficients(): jnp.sum(jnp.square(flattened.astype(jnp.float32)), axis=1)  12 us
  transfers between devices with their start and end apart: 4, of which 4 were waited for; matrix products, arithmetic and copies ran while one was open for 9% of the time, Pallas kernels for 0%

commit v1 on v0

--- a/solution.py
+++ b/solution.py
@@ -113,7 +113,12 @@
     def latent_of(hidden, layer_index):
         partial_value = jnp.dot(
             hidden,
-            lax.all_gather(w_latent[layer_index], "seq", axis=0, tiled=True),
+            jnp.concatenate(
+                lax.all_to_all(
+                    jnp.stack([w_latent[layer_index]] * lax.axis_size("seq")), "seq", 0, 0
+                ),
+                axis=0,
+            ),
             preferred_element_type=jnp.float32,
         )
         summed = taken_together(partial_value, "pd")

time: 584 us -> 1210 us (2.07)
  waiting for transfers between devices: 484 us -> 1060 us
  starting transfers between devices: 3.43 us -> 57.4 us
    all_to_all x0 -> x2, waiting for transfers between devices: none -> 779 us  [latent_of(): lax.all_to_all(jnp.stack([w_latent[layer_index]] * lax.axis_size('seq')),...]
    all_gather x2 -> x0, waiting for transfers between devices: 217 us -> none  [latent_of(): lax.all_gather(w_latent[layer_index], 'seq', axis=0, tiled=True)]
    all_to_all x0 -> x2, starting transfers between devices: none -> 54.1 us  [latent_of(): lax.all_to_all(jnp.stack([w_latent[layer_index]] * lax.axis_size('seq')),...]
  transfers between devices with their start and end apart: 4 -> 4, of which waited for: 4 -> 4; matrix products, arithmetic and copies ran while one was open for 9% -> 1% of each run, Pallas kernels for 0% -> 0%
where the time goes in v1:
time: 1210 us
  waiting for transfers between devices  1060 us (88%)
  starting transfers between devices  57.4 us (5%)
  other arithmetic  26.3 us (2%)
  matrix products  22.4 us (2%)
  between operations  16.5 us (1%)
  local copies, waits for them, and re-layouts  15.1 us (1%)
  blocking collectives  13.1 us (1%)
    all_to_all x2, waiting for transfers between devices, latent_of(): lax.all_to_all(jnp.stack([w_latent[layer_index]] * lax.axis_size('seq')),...  779 us
    all_gather x1, waiting for transfers between devices, on_device(): shard_piece = lax.all_gather(stacked, 'seq', axis=1, tiled=True)  274 us
    all_to_all x2, starting transfers between devices, latent_of(): lax.all_to_all(jnp.stack([w_latent[layer_index]] * lax.axis_size('seq')),...  54.1 us
  transfers between devices with their start and end apart: 4, of which 4 were waited for; matrix products, arithmetic and copies ran while one was open for 1% of the time, Pallas kernels for 0%

profile of v1, /device:TPU:38, one launch (start us, length us, event | category | flops | bytes accessed | tf_op | source)
XLA Modules:
  0.0 1206.5 jit_solution(18174721276216569019)
XLA Ops:
  6.5 0.0 copy-start
  6.6 8.1 multiply_reduce_fusion.1
  14.7 0.0 copy-done
  14.7 0.0 copy-start.7
  14.7 2.1 convolution_bitcast_fusion
  16.8 0.1 reshape.338
  16.9 0.6 broadcast_in_dim.23
  17.6 3.3 all-to-all-start
  20.9 1.3 all-to-all-done
  22.3 2.4 stack.31
  24.7 32.9 %all-to-all-start.1 = ((bf16[32,112,576]{2,1,0:T(8,128)(2,1)}), bf16[32,112,576]{2,1,0:T(8,128)(2,1)}, u32[]{:S(2)}, u32[]{:S(2)}) async-start(bf16[32,112,576]{2,1,0:T(8,128)(2,1)} %stack.31), calls=%async_computation.1 | async-start | bytes 9175040 | tf_op jit(solution)/shard_map/all_to_all | solution.py:117
  57.5 0.0 copy-start.9
  57.6 0.0 copy-start.8
  57.6 7.4 copy.65
  64.9 0.1 reduce_sum.111
  65.0 0.1 reshape.339
  65.1 0.1 copy.68
  65.2 0.1 divide_add_fusion
  65.4 1.7 while.10
  67.2 385.9 %all-to-all-done.1 = bf16[32,112,576]{2,1,0:T(8,128)(2,1)} async-done(((bf16[32,112,576]{2,1,0:T(8,128)(2,1)}), bf16[32,112,576]{2,1,0:T(8,128)(2,1)}, u32[]{:S(2)}, u32[]{:S(2)}) %all-to-all-start.1) | async-done | bytes 4128800 | tf_op jit(solution)/shard_map/all_to_all | solution.py:117
  453.1 8.4 fusion.44
  461.5 0.1 broadcast_in_dim.24
  461.6 4.7 all_to_all.32
  466.3 0.1 reduce_sum.112
  466.4 0.1 multiply_reduce_fusion.3
  466.5 3.3 fusion.100
  469.8 0.0 slice-start
  469.8 0.0 slice-start.1
  469.8 5.7 fusion.56
  475.6 3.7 fusion.57
  479.3 0.0 copy-start.11
  479.3 1.8 multiply_reduce_fusion
  481.1 0.0 copy-done.6
  481.1 2.0 fusion.59
  483.1 0.1 reshape.341
  483.3 3.7 all_to_all.33
  487.0 2.5 stack.37
  489.5 21.2 %all-to-all-start.4 = ((bf16[32,112,576]{2,1,0:T(8,128)(2,1)}), bf16[32,112,576]{2,1,0:T(8,128)(2,1)}, u32[]{:S(2)}, u32[]{:S(2)}) async-start(bf16[32,112,576]{2,1,0:T(8,128)(2,1)} %stack.37), calls=%async_computation.4 | async-start | bytes 9175040 | tf_op jit(solution)/shard_map/all_to_all | solution.py:117
  510.7 0.1 all-gather.2.cloned.1.call-start
  511.5 0.2 fusion.92
  511.7 0.1 compare_bitcast_fusion
  511.8 0.1 convert_bitcast_fusion.4
  511.9 0.1 reshape.342
  512.0 0.1 copy.75
  512.1 0.0 copy-done.10
  512.1 0.1 add_divide_fusion
  512.2 0.1 fusion.101
  512.3 393.6 %all-to-all-done.4 = bf16[32,112,576]{2,1,0:T(8,128)(2,1)} async-done(((bf16[32,112,576]{2,1,0:T(8,128)(2,1)}), bf16[32,112,576]{2,1,0:T(8,128)(2,1)}, u32[]{:S(2)}, u32[]{:S(2)}) %all-to-all-start.4) | async-done | bytes 4128800 | tf_op jit(solution)/shard_map/all_to_all | solution.py:117
  905.9 6.6 fusion.41
  912.5 0.1 broadcast_in_dim.27
  912.6 4.7 all_to_all.34
  917.3 0.1 reduce_sum.116
  917.4 0.1 multiply_reduce_fusion.2
  917.5 0.1 fusion.64
  917.6 0.2 fusion.84
  917.9 0.1 maximum_select_fusion
  918.0 0.9 pad_maximum_fusion.4
  918.9 0.1 all-gather.2.cloned.1.call-update
  918.9 0.7 fusion.97
  920.4 0.6 gather_fusion
  921.0 0.6 fusion.111
  922.9 274.4 %all-gather.2.cloned.1.call-done = bf16[2,8192,576]{1,2,0:T(8,128)(2,1)} async-done(((bf16[2,256,576]{1,2,0:T(8,128)(2,1)}), bf16[2,8192,576]{1,2,0:T(8,128)(2,1)}) %all-gather.2.cloned.1.call-update) | async-done | bytes 18874384 | tf_op jit(solution)/shard_map/all_gather | solution.py:152
  1197.3 1.5 dynamic-slice_select_fusion.1
  1198.8 0.9 pad_maximum_fusion.5
  (106 shorter events, 1.6 us)
Async XLA Ops:
  6.5 8.1 copy-start
  6.6 8.1 copy-start.3
  14.7 6.2 copy-start.7
  17.6 4.7 all-to-all-start
  24.7 428.4 %all-to-all-start.1 = ((bf16[32,112,576]{2,1,0:T(8,128)(2,1)}), bf16[32,112,576]{2,1,0:T(8,128)(2,1)}, u32[]{:S(2)}, u32[]{:S(2)}) async-start(bf16[32,112,576]{2,1,0:T(8,128)(2,1)} %stack.31), calls=%async_computation.1 | async-start | bytes 9175040 | tf_op jit(solution)/shard_map/all_to_all | solution.py:117
  57.5 7.7 copy-start.9
  57.6 7.8 copy-start.8
  469.8 5.8 slice-start
  469.8 5.8 slice-start.1
  475.5 5.5 copy-start.4
  479.2 1.8 copy-start.5
  479.3 1.9 copy-start.6
  479.3 1.8 copy-start.11
  489.5 22.0 %copy-start.2 = (s32[64]{0:T(128)S(1)}, s32[64]{0:T(128)}, u32[]{:S(2)}) copy-start(s32[64]{0:T(128)} %param.21) | copy-start | bytes 772
  489.5 22.6 %copy-start.10 = (f32[4]{0:T(128)S(1)}, f32[4]{0:T(128)}, u32[]{:S(2)}) copy-start(f32[4]{0:T(128)} %param.17) | copy-start | bytes 52
  489.5 416.4 %all-to-all-start.4 = ((bf16[32,112,576]{2,1,0:T(8,128)(2,1)}), bf16[32,112,576]{2,1,0:T(8,128)(2,1)}, u32[]{:S(2)}, u32[]{:S(2)}) async-start(bf16[32,112,576]{2,1,0:T(8,128)(2,1)} %stack.37), calls=%async_computation.4 | async-start | bytes 9175040 | tf_op jit(solution)/shard_map/all_to_all | solution.py:117
  510.7 686.5 %all-gather.2.cloned.1.call-start = ((), (), s32[]{:S(2)}) async-start(), calls=%async_computation.6 | async-start | bytes 19464192 | tf_op jit(solution)/shard_map/all_gather | solution.py:152
  917.3 1.6 copy-start.12
  917.3 282.4 %copy-start.1 = (bf16[4,3584,24]{1,2,0:T(8,128)(2,1)S(1)}, bf16[4,3584,24]{1,2,0:T(8,128)(2,1)}, u32[]{:S(2)}) copy-start(bf16[4,3584,24]{1,2,0:T(8,128)(2,1)} %param.14) | copy-start | bytes 2064388
Sparse Core Ops, SparseCore 0:
  919.0 278.1 all-gather.1
